TPU v7x, 32 devices: a whole 2x2x4 slice. The times are simulated.
32 devices in a mesh: grp: 4 (over y, x), tp: 8 (over z, core).
Axes of the slice: x: 2, y: 2, z: 4, core: 2. Of those that a mesh axis runs over, the one named last changes fastest.
Arguments:
- tokens: bfloat16 [1280, 4096], P(('grp', 'tp')), may hold values from -6 to 6
- norm_gain: float32 [4096], replicated, may hold values from 0.5 to 1.5
- spill_blocks: int32 [1], replicated, may hold values from 0 to 7, as said below
- image_gate: bfloat16 [4096, 11008], P('grp', 'tp'), may hold values from -0.09375 to 0.09375
- image_up: bfloat16 [4096, 11008], P('grp', 'tp'), may hold values from -0.09375 to 0.09375
- image_down: bfloat16 [11008, 4096], P('tp', 'grp'), may hold values from -0.0546875 to 0.0546875
- text_gate: bfloat16 [4096, 11008], P(None, 'tp'), may hold values from -0.09375 to 0.09375
- text_up: bfloat16 [4096, 11008], P(None, 'tp'), may hold values from -0.09375 to 0.09375
- text_down: bfloat16 [11008, 4096], P('tp'), may hold values from -0.0546875 to 0.0546875
Outputs:
- mixed: bfloat16 [1280, 4096], P(('grp', 'tp'))
Inputs may be any that keep to these rules, and one draw needn't show every extreme that they name: `spill_blocks`: 1 distinct indices of 0 to 8 - 1, in increasing order.
All inputs are finite; a program needn't handle non-finite values.
Results may differ from a plain program's by a relative error of at most 0.0046.
Values may be sent and summed in bfloat16 or wider, within the bound.
A program may use at most 256 MiB of HBM per device.

v0:
```python
import jax
import jax.numpy as jnp
from jax import lax
from jax.sharding import PartitionSpec as P

norm_epsilon = 1e-05
bf16 = jnp.bfloat16
f32 = jnp.float32


def on_device(
    tokens, norm_gain, spill_blocks, image_gate, image_up, image_down, text_gate, text_up, text_down
):
    rows, width = tokens.shape
    n_tp = lax.axis_size("tp")
    n_grp = lax.axis_size("grp")
    group = lax.axis_index("grp")
    n_spill = spill_blocks.shape[0]
    in_text = group == n_grp - 1
    kslice = image_gate.shape[0]
    units = image_gate.shape[1]
    wide = tokens.astype(f32)
    scale = lax.rsqrt(jnp.mean(wide * wide, axis=-1, keepdims=True) + norm_epsilon)
    normed = (wide * scale * norm_gain).astype(bf16)
    cols = normed.reshape(rows, n_grp, kslice).transpose(1, 0, 2)
    cols = lax.all_to_all(cols, "grp", 0, 0, tiled=True)
    cols = lax.all_gather(cols, "tp", axis=1, tiled=False)
    image_part = cols[: n_grp - 1].reshape(-1, kslice)
    spill_part = cols[n_grp - 1][spill_blocks].reshape(-1, kslice)
    x = jnp.concatenate([image_part, spill_part], axis=0)
    n_rows = x.shape[0]
    step = 16 * n_grp
    padded = (n_rows + step - 1) // step * step
    x = jnp.pad(x, ((0, padded - n_rows), (0, 0)))
    part_gate = jnp.dot(x, image_gate, preferred_element_type=f32).astype(bf16)
    part_up = jnp.dot(x, image_up, preferred_element_type=f32).astype(bf16)
    gate = lax.psum_scatter(part_gate, "grp", scatter_dimension=0, tiled=True)
    up = lax.psum_scatter(part_up, "grp", scatter_dimension=0, tiled=True)
    piece = lax.all_gather(normed, "tp", axis=0, tiled=True)

    def text_ffn():
        g = jnp.dot(piece, text_gate, preferred_element_type=f32)
        u = jnp.dot(piece, text_up, preferred_element_type=f32)
        h = (jax.nn.silu(g) * u).astype(bf16)
        return jnp.dot(h, text_down, preferred_element_type=f32).astype(bf16)

    text_terms = lax.cond(in_text, text_ffn, lambda: jnp.zeros((n_tp * rows, width), bf16))
    text_out = lax.psum_scatter(text_terms, "tp", scatter_dimension=0, tiled=True)
    hidden = (jax.nn.silu(gate.astype(f32)) * up.astype(f32)).astype(bf16)
    hidden = lax.all_gather(hidden, "grp", axis=0, tiled=True)
    terms = jnp.dot(hidden, image_down, preferred_element_type=f32).astype(bf16)
    image_terms = terms[: (n_grp - 1) * n_tp * rows].reshape(n_grp - 1, n_tp, rows, kslice)
    spill_terms = terms[(n_grp - 1) * n_tp * rows : n_rows].reshape(n_spill, rows, kslice)
    placed = jnp.zeros((n_tp, rows, kslice), bf16).at[spill_blocks].set(spill_terms)
    every = jnp.concatenate([image_terms, placed[None]], axis=0).transpose(1, 0, 2, 3)
    mine = lax.psum_scatter(every.reshape(n_tp, -1, kslice), "tp", scatter_dimension=0, tiled=True)
    mine = mine.reshape(n_grp, rows, kslice)
    back = lax.all_to_all(mine, "grp", 0, 0, tiled=True)
    branch = back.transpose(1, 0, 2).reshape(rows, width)
    is_spill = jnp.any(lax.axis_index("tp") == spill_blocks)
    use_text = jnp.logical_and(in_text, jnp.logical_not(is_spill))
    branch = jnp.where(use_text, text_out, branch)
    return (wide + branch.astype(f32)).astype(bf16)


def solution(mesh):
    in_specs = (
        P(("grp", "tp"), None),
        P(),
        P(),
        P("grp", "tp"),
        P("grp", "tp"),
        P("tp", "grp"),
        P(None, "tp"),
        P(None, "tp"),
        P("tp", None),
    )
    out_specs = P(("grp", "tp"), None)
    return jax.shard_map(
        on_device, mesh=mesh, in_specs=in_specs, out_specs=out_specs, check_vma=False
    )
```

profile of v0, /device:TPU:0, one launch (start us, length us, event | category | flops | bytes accessed | tf_op | source)
XLA Modules:
  0.0 316.9 jit_solution(15081478361410944292)
XLA Ops:
  6.5 0.0 copy-start
  6.5 0.0 all-gather.9.cloned.1.call-start
  6.5 1.3 fusion.10
  7.8 1.1 fusion.12
  9.0 0.0 copy-start.3
  9.0 0.2 reshape.71
  9.2 0.1 copy.27
  9.3 11.6 %all_to_all.10 = bf16[4,40,1024]{2,1,0:T(8,128)(2,1)S(1)} all-to-all(bf16[4,40,1024]{2,1,0:T(8,128)(2,1)S(1)} %copy.27), channel_id=1, replica_groups=mesh['grp'=4,'tp'=8] {'grp'}, dimensions={0} | all-to-all | bytes 655360 | tf_op jit(solution)/shard_map/all_to_all | solution.py:26
  20.9 1.0 copy.28
  21.9 0.0 all-gather.9.cloned.1.call-update
  21.9 0.0 reduce-scatter.7.cloned.1.call-start
  22.6 32.7 %all-gather.9.cloned.1.call-done = bf16[4,320,1024]{2,0,1:T(4,128)(2,1)} async-done(((bf16[4,40,1024]{2,0,1:T(4,128)(2,1)}), bf16[4,320,1024]{2,0,1:T(4,128)(2,1)}) %all-gather.9.cloned.1.call-update) | async-done | bytes 2621456 | tf_op jit(solution)/shard_map/all_gather | solution.py:27
  55.3 0.0 copy-start.2
  55.3 3.4 %slice.47 = bf16[1,320,1024]{2,0,1:T(2,128)(2,1)S(1)} slice(bf16[4,320,1024]{2,0,1:T(4,128)(2,1)} %all-gather.9.cloned.1.call-done), slice={[3:4], [0:320], [0:1024]} | slice | bytes 1310720 | tf_op jit(solution)/shard_map/slice | solution.py:29
  58.7 0.0 copy-done.3
  58.7 0.2 copy.37
  58.9 0.0 copy-done.2
  58.9 0.7 copy.36
  59.7 0.0 copy-start.5
  59.7 1.3 copy-done.5
  61.0 0.0 copy-done
  61.0 5.0 %convolution_convert_fusion.2 = bf16[1024,1376]{0,1:T(8,128)(2,1)} fusion(bf16[1024,1376]{0,1:T(8,128)(2,1)S(1)} %copy-done, bf16[40,1024]{1,0:T(8,128)(2,1)S(1)} %dynamic-slice_bitcast_fusion, bf16[960,1024]{1,0:T(8,128)(2,1)S(1)} %bitcast.35), kind=kOutput, calls=%fused_computation.8 | convolution fusion | flops 2894430208 | bytes 7684096 | tf_op jit(solution)/shard_map/dot_general | solution.py:35
  66.0 0.0 copy-start.6
  66.0 0.0 reduce-scatter.7.cloned.1.call-update
  66.0 0.0 reduce-scatter.9.cloned.1.call-start
  66.1 1.5 copy-done.6
  67.6 6.9 %convolution_convert_fusion.1 = bf16[1024,1376]{0,1:T(8,128)(2,1)} fusion(bf16[1024,1376]{0,1:T(8,128)(2,1)} %param.17, bf16[40,1024]{1,0:T(8,128)(2,1)S(1)} %dynamic-slice_bitcast_fusion, bf16[960,1024]{1,0:T(8,128)(2,1)S(1)} %bitcast.36), kind=kOutput, calls=%fused_computation.7 | convolution fusion | flops 2894430208 | bytes 7684096 | tf_op jit(solution)/shard_map/dot_general | solution.py:36
  74.4 0.0 copy-start.7
  74.4 0.0 reduce-scatter.9.cloned.1.call-update
  74.4 0.0 all-gather.7.cloned.1.call-start
  74.5 32.0 %reduce-scatter.7.cloned.1.call-done = bf16[256,1376]{0,1:T(8,128)(2,1)} async-done(((bf16[1024,1376]{0,1:T(8,128)(2,1)}), bf16[256,1376]{0,1:T(8,128)(2,1)}) %reduce-scatter.7.cloned.1.call-update) | async-done | bytes 704528 | tf_op jit(solution)/shard_map/reduce_scatter | solution.py:37
  106.5 44.3 %reduce-scatter.9.cloned.1.call-done = bf16[256,1376]{0,1:T(8,128)(2,1)} async-done(((bf16[1024,1376]{0,1:T(8,128)(2,1)}), bf16[256,1376]{0,1:T(8,128)(2,1)}) %reduce-scatter.9.cloned.1.call-update) | async-done | bytes 704528 | tf_op jit(solution)/shard_map/reduce_scatter | solution.py:38
  150.8 2.6 fusion.9
  153.4 0.0 all-gather.7.cloned.1.call-update
  153.4 0.0 all-gather.5.cloned.1.call-start
  153.5 0.5 all-gather.5.cloned.1.call-update
  154.0 0.0 reduce-scatter.11.cloned.1.call-start
  154.1 0.0 copy-done.7
  154.1 0.7 and_reduce_fusion
  154.8 39.8 %all-gather.7.cloned.1.call-done = bf16[1024,1376]{0,1:T(8,128)(2,1)} async-done(((bf16[256,1376]{0,1:T(8,128)(2,1)}), bf16[1024,1376]{0,1:T(8,128)(2,1)}) %all-gather.7.cloned.1.call-update) | async-done | bytes 2818064 | tf_op jit(solution)/shard_map/all_gather | solution.py:50
  194.6 6.1 %convolution_convert_fusion.3 = bf16[1024,1024]{1,0:T(8,128)(2,1)S(1)} fusion(bf16[1024,1376]{0,1:T(8,128)(2,1)} %all-gather.7.cloned.1.call-done, bf16[1376,1024]{1,0:T(8,128)(2,1)} %param.18), kind=kOutput, calls=%fused_computation.11 | convolution fusion | flops 2886729728 | bytes 7733248 | tf_op jit(solution)/shard_map/dot_general | solution.py:51
  200.7 0.2 slice.48
  200.9 0.1 broadcast_in_dim.13
  201.0 0.6 fusion.17
  201.6 1.9 pad_maximum_fusion
  203.5 0.0 reduce-scatter.11.cloned.1.call-update
  203.5 0.0 reduce-scatter.5.cloned.1.call-start
  203.5 26.3 %all-gather.5.cloned.1.call-done = bf16[320,4096]{1,0:T(8,128)(2,1)} async-done(((bf16[40,4096]{1,0:T(8,128)(2,1)}), bf16[320,4096]{1,0:T(8,128)(2,1)}) %all-gather.5.cloned.1.call-update) | async-done | bytes 2621456 | tf_op jit(solution)/shard_map/all_gather | solution.py:39
  229.8 1.8 conditional.1
  229.8 1.8 broadcast.40
  231.6 0.0 copy-start.4
  231.6 0.0 copy-start.1
  231.6 0.0 reduce-scatter.5.cloned.1.call-update
  231.6 37.3 %reduce-scatter.11.cloned.1.call-done = bf16[1,160,1024]{2,1,0:T(8,128)(2,1)} async-done(((bf16[8,160,1024]{2,1,0:T(8,128)(2,1)}), bf16[1,160,1024]{2,1,0:T(8,128)(2,1)}) %reduce-scatter.11.cloned.1.call-update) | async-done | bytes 327696 | tf_op jit(solution)/shard_map/reduce_scatter | solution.py:56
  268.9 3.7 %all-to-all-start.1 = ((bf16[4,40,1024]{2,1,0:T(8,128)(2,1)}), bf16[4,40,1024]{2,1,0:T(8,128)(2,1)S(1)}, u32[]{:S(2)}, u32[]{:S(2)}) async-start(bf16[4,40,1024]{2,1,0:T(8,128)(2,1)} %bitcast.41), calls=%async_computation.5 | async-start | bytes 655360 | tf_op jit(solution)/shard_map/all_to_all | solution.py:58
  272.7 5.5 %all-to-all-done.1 = bf16[4,40,1024]{2,1,0:T(8,128)(2,1)S(1)} async-done(((bf16[4,40,1024]{2,1,0:T(8,128)(2,1)}), bf16[4,40,1024]{2,1,0:T(8,128)(2,1)S(1)}, u32[]{:S(2)}, u32[]{:S(2)}) %all-to-all-start.1) | async-done | bytes 327712 | tf_op jit(solution)/shard_map/all_to_all | solution.py:58
  278.2 0.7 copy.38
  279.0 29.3 %reduce-scatter.5.cloned.1.call-done = bf16[40,4096]{1,0:T(8,128)(2,1)} async-done(((bf16[320,4096]{1,0:T(8,128)(2,1)}), bf16[40,4096]{1,0:T(8,128)(2,1)}) %reduce-scatter.5.cloned.1.call-update) | async-done | bytes 327696 | tf_op jit(solution)/shard_map/reduce_scatter | solution.py:48
  308.2 0.0 copy-done.4
  308.2 1.8 fusion.13
  310.0 0.0 copy-done.1
  (2 shorter events, 0.0 us)
Async XLA Ops:
  6.5 54.5 %copy-start = (bf16[1024,1376]{0,1:T(8,128)(2,1)S(1)}, bf16[1024,1376]{0,1:T(8,128)(2,1)}, u32[]{:S(2)}) copy-start(bf16[1024,1376]{0,1:T(8,128)(2,1)} %param.16) | copy-start | bytes 8454148
  6.5 48.8 %all-gather.9.cloned.1.call-start = ((), (), s32[]{:S(2)}) async-start(), calls=%async_computation.12 | async-start | bytes 2949120 | tf_op jit(solution)/shard_map/all_gather | solution.py:27
  9.0 49.7 %copy-start.3 = (bf16[40,4096]{1,0:T(8,128)(2,1)}, bf16[40,4096]{1,0:T(8,128)(2,1)S(1)}, u32[]{:S(2)}) copy-start(bf16[40,4096]{1,0:T(8,128)(2,1)S(1)} %fusion.12) | copy-start | bytes 983044
  21.9 84.6 %reduce-scatter.7.cloned.1.call-start = ((), (), s32[]{:S(2)}) async-start(), calls=%async_computation.8 | async-start | bytes 3522560 | tf_op jit(solution)/shard_map/reduce_scatter | solution.py:37
  55.3 3.6 %copy-start.2 = (bf16[4,320,1024]{2,0,1:T(4,128)(2,1)S(1)}, bf16[4,320,1024]{2,0,1:T(4,128)(2,1)}, u32[]{:S(2)}) copy-start(bf16[4,320,1024]{2,0,1:T(4,128)(2,1)} %all-gather.9.cloned.1.call-done) | copy-start | bytes 7864324
  59.7 1.3 copy-start.5
  66.0 1.5 copy-start.6
  66.0 84.7 %reduce-scatter.9.cloned.1.call-start = ((), (), s32[]{:S(2)}) async-start(), calls=%async_computation.9 | async-start | bytes 3522560 | tf_op jit(solution)/shard_map/reduce_scatter | solution.py:38
  74.4 79.6 %copy-start.7 = (s32[3]{0:T(128)S(1)}, s32[3]{0:T(128)}, u32[]{:S(2)}) copy-start(s32[3]{0:T(128)} %constant.55.clone.1) | copy-start | bytes 40
  74.4 120.1 %all-gather.7.cloned.1.call-start = ((), (), s32[]{:S(2)}) async-start(), calls=%async_computation.10 | async-start | bytes 3522560 | tf_op jit(solution)/shard_map/all_gather | solution.py:50
  153.4 76.4 %all-gather.5.cloned.1.call-start = ((), (), s32[]{:S(2)}) async-start(), calls=%async_computation.6 | async-start | bytes 2949120 | tf_op jit(solution)/shard_map/all_gather | solution.py:39
  154.0 114.9 %reduce-scatter.11.cloned.1.call-start = ((), (), s32[]{:S(2)}) async-start(), calls=%async_computation.11 | async-start | bytes 2949120 | tf_op jit(solution)/shard_map/reduce_scatter | solution.py:56
  203.5 104.7 %reduce-scatter.5.cloned.1.call-start = ((), (), s32[]{:S(2)}) async-start(), calls=%async_computation.7 | async-start | bytes 2949120 | tf_op jit(solution)/shard_map/reduce_scatter | solution.py:48
  231.6 76.6 %copy-start.4 = (bf16[40,4096]{1,0:T(8,128)(2,1)S(1)}, bf16[40,4096]{1,0:T(8,128)(2,1)}, u32[]{:S(2)}) copy-start(bf16[40,4096]{1,0:T(8,128)(2,1)} %param.13) | copy-start | bytes 983044
  231.6 78.4 %copy-start.1 = (bf16[1024,1376]{0,1:T(8,128)(2,1)S(1)}, bf16[1024,1376]{0,1:T(8,128)(2,1)}, u32[]{:S(2)}) copy-start(bf16[1024,1376]{0,1:T(8,128)(2,1)} %param.16) | copy-start | bytes 8454148
  268.9 9.3 %all-to-all-start.1 = ((bf16[4,40,1024]{2,1,0:T(8,128)(2,1)}), bf16[4,40,1024]{2,1,0:T(8,128)(2,1)S(1)}, u32[]{:S(2)}, u32[]{:S(2)}) async-start(bf16[4,40,1024]{2,1,0:T(8,128)(2,1)} %bitcast.41), calls=%async_computation.5 | async-start | bytes 655360 | tf_op jit(solution)/shard_map/all_to_all | solution.py:58
Sparse Core Ops, SparseCore 0:
  22.1 33.2 all-gather.8
  66.2 40.3 reduce-scatter.6
  109.6 41.1 reduce-scatter.8
  153.5 41.0 all-gather.6
  196.1 33.6 all-gather.4
  231.9 36.9 reduce-scatter.10
  271.2 36.9 reduce-scatter.4
where the time goes:
time: 317 us
  waiting for transfers between devices  248 us (78%)
  matrix products  18 us (6%)
  between operations  14.3 us (5%)
  blocking collectives  11.6 us (4%)
  local copies, waits for them, and re-layouts  11.2 us (4%)
  other arithmetic  10.1 us (3%)
  starting transfers between devices  3.99 us (1%)
    reduce_scatter x1, waiting for transfers between devices, on_device(): up = lax.psum_scatter(part_up, 'grp', scatter_dimension=0, tiled=True)  44.3 us
    all_gather x1, waiting for transfers between devices, on_device(): hidden = lax.all_gather(hidden, 'grp', axis=0, tiled=True)  39.8 us
    reduce_scatter x1, waiting for transfers between devices, on_device(): lax.psum_scatter(every.reshape(n_tp, -1, kslice), 'tp', scatter_dimension...  37.3 us
    all_gather x1, waiting for transfers between devices, on_device(): cols = lax.all_gather(cols, 'tp', axis=1, tiled=False)  32.7 us
    reduce_scatter x1, waiting for transfers between devices, on_device(): gate = lax.psum_scatter(part_gate, 'grp', scatter_dimension=0, tiled=True)  32 us
    reduce_scatter x1, waiting for transfers between devices, on_device(): lax.psum_scatter(text_terms, 'tp', scatter_dimension=0, tiled=True)  29.3 us
    all_gather x1, waiting for transfers between devices, on_device(): piece = lax.all_gather(normed, 'tp', axis=0, tiled=True)  26.3 us
    all_to_all x1, blocking collectives, on_device(): cols = lax.all_to_all(cols, 'grp', 0, 0, tiled=True)  11.6 us
  transfers between devices with their start and end apart: 8, of which 8 were waited for; matrix products, arithmetic and copies ran while one was open for 6% of the time, Pallas kernels for 0%

commit v1 on v0

--- a/solution.py
+++ b/solution.py
@@ -36,7 +36,13 @@
     part_up = jnp.dot(x, image_up, preferred_element_type=f32).astype(bf16)
     gate = lax.psum_scatter(part_gate, "grp", scatter_dimension=0, tiled=True)
     up = lax.psum_scatter(part_up, "grp", scatter_dimension=0, tiled=True)
-    piece = lax.all_gather(normed, "tp", axis=0, tiled=True)
+    size = lax.axis_size("tp")
+    held, blocks = (normed, [normed])
+    for _ in range(size - 1):
+        held = lax.ppermute(held, "tp", [(i, (i + 1) % size) for i in range(size)])
+        blocks.insert(0, held)
+    row_of_blocks = jnp.concatenate(blocks, axis=0)
+    piece = jnp.roll(row_of_blocks, (lax.axis_index("tp") + 1) * normed.shape[0], axis=0)
 
     def text_ffn():
         g = jnp.dot(piece, text_gate, preferred_element_type=f32)

time: 317 us -> 290 us (0.915)
  waiting for transfers between devices: 248 us -> 209 us
  local copies, waits for them, and re-layouts: 11.2 us -> 20.3 us
    ppermute x0 -> x7, waiting for transfers between devices: none -> 48.8 us  [on_device(): held = lax.ppermute(held, 'tp', [(i, (i + 1) % size) for i in range(size)])]
    all_gather x1, waiting for transfers between devices: 39.8 us -> 3.29 us  [on_device(): hidden = lax.all_gather(hidden, 'grp', axis=0, tiled=True)]
    all_gather x1 -> x0, waiting for transfers between devices: 26.3 us -> none  [on_device(): piece = lax.all_gather(normed, 'tp', axis=0, tiled=True)]
    reduce_scatter x1, waiting for transfers between devices: 32 us -> 16.6 us  [on_device(): gate = lax.psum_scatter(part_gate, 'grp', scatter_dimension=0, tiled=True)]
    unnamed x18 -> x50, local copies, waits for them, and re-layouts: 3.73 us -> 12.8 us
    reduce_scatter x1, waiting for transfers between devices: 37.3 us -> 28.2 us  [on_device(): lax.psum_scatter(every.reshape(n_tp, -1, kslice), 'tp', scatter_dimension...]
  transfers between devices with their start and end apart: 8 -> 14, of which waited for: 8 -> 13; matrix products, arithmetic and copies ran while one was open for 6% -> 9% of each run, Pallas kernels for 0% -> 0%
where the time goes in v1:
time: 290 us; the launch traced here: 289 us
  waiting for transfers between devices  209 us (72%)
  local copies, waits for them, and re-layouts  20.3 us (7%)
  matrix products  18.3 us (6%)
  between operations  14.3 us (5%)
  other arithmetic  11.7 us (4%)
  blocking collectives  11.6 us (4%)
  starting transfers between devices  4.19 us (1%)
    ppermute x7, waiting for transfers between devices, on_device(): held = lax.ppermute(held, 'tp', [(i, (i + 1) % size) for i in range(size)])  48.8 us
    reduce_scatter x1, waiting for transfers between devices, on_device(): up = lax.psum_scatter(part_up, 'grp', scatter_dimension=0, tiled=True)  44.3 us
    all_gather x1, waiting for transfers between devices, on_device(): cols = lax.all_gather(cols, 'tp', axis=1, tiled=False)  32.7 us
    reduce_scatter x1, waiting for transfers between devices, on_device(): lax.psum_scatter(text_terms, 'tp', scatter_dimension=0, tiled=True)  29.3 us
    reduce_scatter x1, waiting for transfers between devices, on_device(): lax.psum_scatter(every.reshape(n_tp, -1, kslice), 'tp', scatter_dimension...  28.2 us
    reduce_scatter x1, waiting for transfers between devices, on_device(): gate = lax.psum_scatter(part_gate, 'grp', scatter_dimension=0, tiled=True)  16.6 us
    unnamed x50, local copies, waits for them, and re-layouts  12.8 us
    all_to_all x1, blocking collectives, on_device(): cols = lax.all_to_all(cols, 'grp', 0, 0, tiled=True)  11.6 us
  transfers between devices with their start and end apart: 14, of which 13 were waited for; matrix products, arithmetic and copies ran while one was open for 9% of the time, Pallas kernels for 0%

profile of v1, /device:TPU:0, one launch (start us, length us, event | category | flops | bytes accessed | tf_op | source)
XLA Modules:
  0.0 289.2 jit_solution(699832604901520293)
XLA Ops:
  6.5 1.3 fusion.23
  7.8 1.1 fusion.25
  9.0 0.2 reshape.71
  9.2 0.1 copy.27
  9.3 11.6 %all_to_all.10 = bf16[4,40,1024]{2,1,0:T(8,128)(2,1)S(1)} all-to-all(bf16[4,40,1024]{2,1,0:T(8,128)(2,1)S(1)} %copy.27), channel_id=1, replica_groups=mesh['grp'=4,'tp'=8] {'grp'}, dimensions={0} | all-to-all | bytes 655360 | tf_op jit(solution)/shard_map/all_to_all | solution.py:26
  20.9 1.0 copy.28
  21.9 0.0 all-gather.6.cloned.1.call-update
  21.9 0.0 reduce-scatter.7.cloned.1.call-start
  22.6 32.7 %all-gather.6.cloned.1.call-done = bf16[4,320,1024]{2,0,1:T(4,128)(2,1)} async-done(((bf16[4,40,1024]{2,0,1:T(4,128)(2,1)}), bf16[4,320,1024]{2,0,1:T(4,128)(2,1)}) %all-gather.6.cloned.1.call-update) | async-done | bytes 2621456 | tf_op jit(solution)/shard_map/all_gather | solution.py:27
  55.3 3.4 %slice.47 = bf16[1,320,1024]{2,0,1:T(2,128)(2,1)S(1)} slice(bf16[4,320,1024]{2,0,1:T(4,128)(2,1)} %all-gather.6.cloned.1.call-done), slice={[3:4], [0:320], [0:1024]} | slice | bytes 1310720 | tf_op jit(solution)/shard_map/slice | solution.py:29
  58.7 0.2 copy.37
  58.9 0.7 copy.36
  59.7 1.2 copy-done.4
  60.9 5.0 %convolution_convert_fusion.2 = bf16[1024,1376]{0,1:T(8,128)(2,1)} fusion(bf16[1024,1376]{0,1:T(8,128)(2,1)S(1)} %copy-done, bf16[40,1024]{1,0:T(8,128)(2,1)S(1)} %dynamic-slice_bitcast_fusion, bf16[960,1024]{1,0:T(8,128)(2,1)S(1)} %bitcast.33), kind=kOutput, calls=%fused_computation.18 | convolution fusion | flops 2894430208 | bytes 7684096 | tf_op jit(solution)/shard_map/dot_general | solution.py:35
  66.0 0.0 reduce-scatter.9.cloned.1.call-start
  66.0 7.1 %convolution_convert_fusion.1 = bf16[1024,1376]{0,1:T(8,128)(2,1)} fusion(bf16[1024,1376]{0,1:T(8,128)(2,1)} %param.17, bf16[40,1024]{1,0:T(8,128)(2,1)S(1)} %dynamic-slice_bitcast_fusion, bf16[960,1024]{1,0:T(8,128)(2,1)} %bitcast.34), kind=kOutput, calls=%fused_computation.17 | convolution fusion | flops 2894430208 | bytes 7684096 | tf_op jit(solution)/shard_map/dot_general | solution.py:36
  73.1 0.0 reduce-scatter.9.cloned.1.call-update
  73.1 0.0 all-gather.4.cloned.1.call-start
  73.2 0.3 collective-permute-start
  73.5 8.1 %collective-permute-done = bf16[40,4096]{1,0:T(8,128)(2,1)S(1)} collective-permute-done((bf16[40,4096]{1,0:T(8,128)(2,1)S(1)}, bf16[40,4096]{1,0:T(8,128)(2,1)S(1)}, u32[]{:S(2)}, u32[]{:S(2)}) %collective-permute-start) | collective-permute-done | bytes 327712 | tf_op jit(solution)/shard_map/ppermute | solution.py:42
  81.5 8.3 %collective-permute-done.1 = bf16[40,4096]{1,0:T(8,128)(2,1)S(1)} collective-permute-done((bf16[40,4096]{1,0:T(8,128)(2,1)S(1)}, bf16[40,4096]{1,0:T(8,128)(2,1)S(1)}, u32[]{:S(2)}, u32[]{:S(2)}) %collective-permute-start.1) | collective-permute-done | bytes 327712 | tf_op jit(solution)/shard_map/ppermute | solution.py:42
  89.8 16.6 %reduce-scatter.7.cloned.1.call-done = bf16[256,1376]{0,1:T(8,128)(2,1)} async-done(((bf16[1024,1376]{0,1:T(8,128)(2,1)}), bf16[256,1376]{0,1:T(8,128)(2,1)}) %reduce-scatter.7.cloned.1.call-update) | async-done | bytes 704528 | tf_op jit(solution)/shard_map/reduce_scatter | solution.py:37
  106.5 44.3 %reduce-scatter.9.cloned.1.call-done = bf16[256,1376]{0,1:T(8,128)(2,1)} async-done(((bf16[1024,1376]{0,1:T(8,128)(2,1)}), bf16[256,1376]{0,1:T(8,128)(2,1)}) %reduce-scatter.9.cloned.1.call-update) | async-done | bytes 704528 | tf_op jit(solution)/shard_map/reduce_scatter | solution.py:38
  150.7 2.6 fusion.22
  153.4 0.0 all-gather.4.cloned.1.call-update
  153.4 0.0 reduce-scatter.11.cloned.1.call-start
  153.4 0.1 collective-permute-start.3
  153.5 8.3 %collective-permute-done.3 = bf16[40,4096]{1,0:T(8,128)(2,1)S(1)} collective-permute-done((bf16[40,4096]{1,0:T(8,128)(2,1)S(1)}, bf16[40,4096]{1,0:T(8,128)(2,1)S(1)}, u32[]{:S(2)}, u32[]{:S(2)}) %collective-permute-start.3) | collective-permute-done | bytes 327712 | tf_op jit(solution)/shard_map/ppermute | solution.py:42
  161.8 8.3 %collective-permute-done.4 = bf16[40,4096]{1,0:T(8,128)(2,1)S(1)} collective-permute-done((bf16[40,4096]{1,0:T(8,128)(2,1)S(1)}, bf16[40,4096]{1,0:T(8,128)(2,1)S(1)}, u32[]{:S(2)}, u32[]{:S(2)}) %collective-permute-start.4) | collective-permute-done | bytes 327712 | tf_op jit(solution)/shard_map/ppermute | solution.py:42
  170.1 8.3 %collective-permute-done.5 = bf16[40,4096]{1,0:T(8,128)(2,1)S(1)} collective-permute-done((bf16[40,4096]{1,0:T(8,128)(2,1)S(1)}, bf16[40,4096]{1,0:T(8,128)(2,1)S(1)}, u32[]{:S(2)}, u32[]{:S(2)}) %collective-permute-start.5) | collective-permute-done | bytes 327712 | tf_op jit(solution)/shard_map/ppermute | solution.py:42
  178.4 0.7 and_reduce_fusion
  179.1 7.6 %collective-permute-done.6 = bf16[40,4096]{1,0:T(8,128)(2,1)S(1)} collective-permute-done((bf16[40,4096]{1,0:T(8,128)(2,1)S(1)}, bf16[40,4096]{1,0:T(8,128)(2,1)S(1)}, u32[]{:S(2)}, u32[]{:S(2)}) %collective-permute-start.6) | collective-permute-done | bytes 327712 | tf_op jit(solution)/shard_map/ppermute | solution.py:42
  186.7 0.8 constant_dynamic-update-slice_fusion.15
  187.5 0.7 constant_dynamic-update-slice_fusion.14
  188.2 0.8 constant_dynamic-update-slice_fusion.13
  189.0 0.8 constant_dynamic-update-slice_fusion.12
  189.7 0.8 constant_dynamic-update-slice_fusion.11
  190.5 0.8 constant_dynamic-update-slice_fusion.10
  191.2 3.3 %all-gather.4.cloned.1.call-done = bf16[1024,1376]{0,1:T(8,128)(2,1)} async-done(((bf16[256,1376]{0,1:T(8,128)(2,1)}), bf16[1024,1376]{0,1:T(8,128)(2,1)}) %all-gather.4.cloned.1.call-update) | async-done | bytes 2818064 | tf_op jit(solution)/shard_map/all_gather | solution.py:56
  194.5 6.1 %convolution_convert_fusion.3 = bf16[1024,1024]{1,0:T(8,128)(2,1)S(1)} fusion(bf16[1024,1376]{0,1:T(8,128)(2,1)} %all-gather.4.cloned.1.call-done, bf16[1376,1024]{1,0:T(8,128)(2,1)} %param.18), kind=kOutput, calls=%fused_computation.21 | convolution fusion | flops 2886729728 | bytes 7733248 | tf_op jit(solution)/shard_map/dot_general | solution.py:57
  200.7 0.2 slice.48
  200.9 0.1 broadcast_in_dim.13
  200.9 0.6 fusion.30
  201.6 1.8 pad_maximum_fusion
  203.4 0.0 reduce-scatter.11.cloned.1.call-update
  203.4 0.0 reduce-scatter.5.cloned.1.call-start
  203.4 0.7 constant_dynamic-update-slice_fusion.9
  204.2 0.9 constant_dynamic-update-slice_fusion.8
  205.1 0.8 constant_dynamic-update-slice_fusion.7
  205.8 0.7 constant_dynamic-update-slice_fusion.6
  206.6 0.7 constant_dynamic-update-slice_fusion.5
  207.3 0.7 constant_dynamic-update-slice_fusion.4
  208.1 0.7 constant_dynamic-update-slice_fusion.3
  208.8 0.8 constant_dynamic-update-slice_fusion.2
  209.6 0.7 constant_dynamic-update-slice_fusion.1
  210.3 0.9 constant_dynamic-update-slice_fusion
  211.2 1.9 conditional.1
  211.2 1.9 broadcast.43
  213.1 28.2 %reduce-scatter.11.cloned.1.call-done = bf16[1,160,1024]{2,1,0:T(8,128)(2,1)} async-done(((bf16[8,160,1024]{2,1,0:T(8,128)(2,1)}), bf16[1,160,1024]{2,1,0:T(8,128)(2,1)}) %reduce-scatter.11.cloned.1.call-update) | async-done | bytes 327696 | tf_op jit(solution)/shard_map/reduce_scatter | solution.py:62
  241.4 3.6 %all-to-all-start.1 = ((bf16[4,40,1024]{2,1,0:T(8,128)(2,1)}), bf16[4,40,1024]{2,1,0:T(8,128)(2,1)S(1)}, u32[]{:S(2)}, u32[]{:S(2)}) async-start(bf16[4,40,1024]{2,1,0:T(8,128)(2,1)} %bitcast.39), calls=%async_computation.5 | async-start | bytes 655360 | tf_op jit(solution)/shard_map/all_to_all | solution.py:64
  245.0 5.5 %all-to-all-done.1 = bf16[4,40,1024]{2,1,0:T(8,128)(2,1)S(1)} async-done(((bf16[4,40,1024]{2,1,0:T(8,128)(2,1)}), bf16[4,40,1024]{2,1,0:T(8,128)(2,1)S(1)}, u32[]{:S(2)}, u32[]{:S(2)}) %all-to-all-start.1) | async-done | bytes 327712 | tf_op jit(solution)/shard_map/all_to_all | solution.py:64
  250.5 0.7 copy.38
  251.3 29.3 %reduce-scatter.5.cloned.1.call-done = bf16[40,4096]{1,0:T(8,128)(2,1)} async-done(((bf16[320,4096]{1,0:T(8,128)(2,1)}), bf16[40,4096]{1,0:T(8,128)(2,1)}) %reduce-scatter.5.cloned.1.call-update) | async-done | bytes 327696 | tf_op jit(solution)/shard_map/reduce_scatter | solution.py:54
  280.6 1.8 fusion.26
  (44 shorter events, 0.1 us)
Async XLA Ops:
  6.5 54.4 %copy-start = (bf16[1024,1376]{0,1:T(8,128)(2,1)S(1)}, bf16[1024,1376]{0,1:T(8,128)(2,1)}, u32[]{:S(2)}) copy-start(bf16[1024,1376]{0,1:T(8,128)(2,1)} %param.16) | copy-start | bytes 8454148
  6.5 48.8 %all-gather.6.cloned.1.call-start = ((), (), s32[]{:S(2)}) async-start(), calls=%async_computation.11 | async-start | bytes 2949120 | tf_op jit(solution)/shard_map/all_gather | solution.py:27
  21.9 84.5 %reduce-scatter.7.cloned.1.call-start = ((), (), s32[]{:S(2)}) async-start(), calls=%async_computation.7 | async-start | bytes 3522560 | tf_op jit(solution)/shard_map/reduce_scatter | solution.py:37
  55.3 3.6 %copy-start.3 = (bf16[4,320,1024]{2,0,1:T(4,128)(2,1)S(1)}, bf16[4,320,1024]{2,0,1:T(4,128)(2,1)}, u32[]{:S(2)}) copy-start(bf16[4,320,1024]{2,0,1:T(4,128)(2,1)} %all-gather.6.cloned.1.call-done) | copy-start | bytes 7864324
  59.6 1.3 copy-start.4
  66.0 84.7 %reduce-scatter.9.cloned.1.call-start = ((), (), s32[]{:S(2)}) async-start(), calls=%async_computation.8 | async-start | bytes 3522560 | tf_op jit(solution)/shard_map/reduce_scatter | solution.py:38
  73.1 105.3 %copy-start.16 = (s32[3]{0:T(128)S(1)}, s32[3]{0:T(128)}, u32[]{:S(2)}) copy-start(s32[3]{0:T(128)} %constant.94.clone.1) | copy-start | bytes 40
  73.1 121.4 %all-gather.4.cloned.1.call-start = ((), (), s32[]{:S(2)}) async-start(), calls=%async_computation.9 | async-start | bytes 3522560 | tf_op jit(solution)/shard_map/all_gather | solution.py:56
  73.2 8.3 %collective-permute-start = (bf16[40,4096]{1,0:T(8,128)(2,1)S(1)}, bf16[40,4096]{1,0:T(8,128)(2,1)S(1)}, u32[]{:S(2)}, u32[]{:S(2)}) collective-permute-start(bf16[40,4096]{1,0:T(8,128)(2,1)S(1)} %fusion.25), channel_id=1, source_target_pairs={{0,1},{1,2},{2,3},{3,4},{4,5},{5,6},{6,7},{7,0},{8,9},{9,10},{10,1... | collective-permute-start | bytes 983048 | tf_op jit(solution)/shard_map/ppermute | solution.py:42
  81.5 8.3 %collective-permute-start.1 = (bf16[40,4096]{1,0:T(8,128)(2,1)S(1)}, bf16[40,4096]{1,0:T(8,128)(2,1)S(1)}, u32[]{:S(2)}, u32[]{:S(2)}) collective-permute-start(bf16[40,4096]{1,0:T(8,128)(2,1)S(1)} %collective-permute-done), channel_id=1, source_target_pairs={{0,1},{1,2},{2,3},{3,4},{4,5},{5,6},{6,7},{7,0},{8,9},{9,10},{10,1... | collective-permute-start | bytes 983048 | tf_op jit(solution)/shard_map/ppermute | solution.py:42
  89.8 110.8 %copy-start.5 = (bf16[40,4096]{1,0:T(8,128)(2,1)}, bf16[40,4096]{1,0:T(8,128)(2,1)S(1)}, u32[]{:S(2)}) copy-start(bf16[40,4096]{1,0:T(8,128)(2,1)S(1)} %collective-permute-done.1) | copy-start | bytes 983044
  89.8 63.6 %collective-permute-start.2 = (bf16[40,4096]{1,0:T(8,128)(2,1)S(1)}, bf16[40,4096]{1,0:T(8,128)(2,1)S(1)}, u32[]{:S(2)}, u32[]{:S(2)}) collective-permute-start(bf16[40,4096]{1,0:T(8,128)(2,1)S(1)} %collective-permute-done.1), channel_id=1, source_target_pairs={{0,1},{1,2},{2,3},{3,4},{4,5},{5,6},{6,7},{7,0},{8,9},{9,10},{10,1... | collective-permute-start | bytes 983048 | tf_op jit(solution)/shard_map/ppermute | solution.py:42
  153.4 88.0 %reduce-scatter.11.cloned.1.call-start = ((), (), s32[]{:S(2)}) async-start(), calls=%async_computation.10 | async-start | bytes 2949120 | tf_op jit(solution)/shard_map/reduce_scatter | solution.py:62
  153.4 41.1 %copy-start.7 = (bf16[40,4096]{1,0:T(8,128)(2,1)}, bf16[40,4096]{1,0:T(8,128)(2,1)S(1)}, u32[]{:S(2)}) copy-start(bf16[40,4096]{1,0:T(8,128)(2,1)S(1)} %collective-permute-done.2) | copy-start | bytes 983044
  153.4 8.3 %collective-permute-start.3 = (bf16[40,4096]{1,0:T(8,128)(2,1)S(1)}, bf16[40,4096]{1,0:T(8,128)(2,1)S(1)}, u32[]{:S(2)}, u32[]{:S(2)}) collective-permute-start(bf16[40,4096]{1,0:T(8,128)(2,1)S(1)} %collective-permute-done.2), channel_id=1, source_target_pairs={{0,1},{1,2},{2,3},{3,4},{4,5},{5,6},{6,7},{7,0},{8,9},{9,10},{10,1... | collective-permute-start | bytes 983048 | tf_op jit(solution)/shard_map/ppermute | solution.py:42
  161.8 32.7 %copy-start.9 = (bf16[40,4096]{1,0:T(8,128)(2,1)}, bf16[40,4096]{1,0:T(8,128)(2,1)S(1)}, u32[]{:S(2)}) copy-start(bf16[40,4096]{1,0:T(8,128)(2,1)S(1)} %collective-permute-done.3) | copy-start | bytes 983044
  161.8 8.3 %collective-permute-start.4 = (bf16[40,4096]{1,0:T(8,128)(2,1)S(1)}, bf16[40,4096]{1,0:T(8,128)(2,1)S(1)}, u32[]{:S(2)}, u32[]{:S(2)}) collective-permute-start(bf16[40,4096]{1,0:T(8,128)(2,1)S(1)} %collective-permute-done.3), channel_id=1, source_target_pairs={{0,1},{1,2},{2,3},{3,4},{4,5},{5,6},{6,7},{7,0},{8,9},{9,10},{10,1... | collective-permute-start | bytes 983048 | tf_op jit(solution)/shard_map/ppermute | solution.py:42
  170.1 24.4 %copy-start.11 = (bf16[40,4096]{1,0:T(8,128)(2,1)}, bf16[40,4096]{1,0:T(8,128)(2,1)S(1)}, u32[]{:S(2)}) copy-start(bf16[40,4096]{1,0:T(8,128)(2,1)S(1)} %collective-permute-done.4) | copy-start | bytes 983044
  170.1 8.3 %collective-permute-start.5 = (bf16[40,4096]{1,0:T(8,128)(2,1)S(1)}, bf16[40,4096]{1,0:T(8,128)(2,1)S(1)}, u32[]{:S(2)}, u32[]{:S(2)}) collective-permute-start(bf16[40,4096]{1,0:T(8,128)(2,1)S(1)} %collective-permute-done.4), channel_id=1, source_target_pairs={{0,1},{1,2},{2,3},{3,4},{4,5},{5,6},{6,7},{7,0},{8,9},{9,10},{10,1... | collective-permute-start | bytes 983048 | tf_op jit(solution)/shard_map/ppermute | solution.py:42
  178.4 16.1 %copy-start.13 = (bf16[40,4096]{1,0:T(8,128)(2,1)}, bf16[40,4096]{1,0:T(8,128)(2,1)S(1)}, u32[]{:S(2)}) copy-start(bf16[40,4096]{1,0:T(8,128)(2,1)S(1)} %collective-permute-done.5) | copy-start | bytes 983044
  178.4 8.3 %collective-permute-start.6 = (bf16[40,4096]{1,0:T(8,128)(2,1)S(1)}, bf16[40,4096]{1,0:T(8,128)(2,1)S(1)}, u32[]{:S(2)}, u32[]{:S(2)}) collective-permute-start(bf16[40,4096]{1,0:T(8,128)(2,1)S(1)} %collective-permute-done.5), channel_id=1, source_target_pairs={{0,1},{1,2},{2,3},{3,4},{4,5},{5,6},{6,7},{7,0},{8,9},{9,10},{10,1... | collective-permute-start | bytes 983048 | tf_op jit(solution)/shard_map/ppermute | solution.py:42
  201.5 2.6 copy-start.2
  201.5 2.6 copy-start.15
  203.3 2.5 copy-start.14
  203.3 3.3 %copy-start.12 = (bf16[40,4096]{1,0:T(8,128)(2,1)S(1)}, bf16[40,4096]{1,0:T(8,128)(2,1)}, u32[]{:S(2)}) copy-start(bf16[40,4096]{1,0:T(8,128)(2,1)} %copy-done.11) | copy-start | bytes 983044
  203.3 4.0 %copy-start.10 = (bf16[40,4096]{1,0:T(8,128)(2,1)S(1)}, bf16[40,4096]{1,0:T(8,128)(2,1)}, u32[]{:S(2)}) copy-start(bf16[40,4096]{1,0:T(8,128)(2,1)} %copy-done.9) | copy-start | bytes 983044
  203.3 4.7 %copy-start.8 = (bf16[40,4096]{1,0:T(8,128)(2,1)S(1)}, bf16[40,4096]{1,0:T(8,128)(2,1)}, u32[]{:S(2)}) copy-start(bf16[40,4096]{1,0:T(8,128)(2,1)} %copy-done.7) | copy-start | bytes 983044
  203.3 5.5 %copy-start.6 = (bf16[40,4096]{1,0:T(8,128)(2,1)S(1)}, bf16[40,4096]{1,0:T(8,128)(2,1)}, u32[]{:S(2)}) copy-start(bf16[40,4096]{1,0:T(8,128)(2,1)} %copy-done.5) | copy-start | bytes 983044
  203.4 77.2 %reduce-scatter.5.cloned.1.call-start = ((), (), s32[]{:S(2)}) async-start(), calls=%async_computation.6 | async-start | bytes 2949120 | tf_op jit(solution)/shard_map/reduce_scatter | solution.py:54
  213.1 69.3 %copy-start.1 = (bf16[1024,1376]{0,1:T(8,128)(2,1)S(1)}, bf16[1024,1376]{0,1:T(8,128)(2,1)}, u32[]{:S(2)}) copy-start(bf16[1024,1376]{0,1:T(8,128)(2,1)} %param.16) | copy-start | bytes 8454148
  241.4 9.2 %all-to-all-start.1 = ((bf16[4,40,1024]{2,1,0:T(8,128)(2,1)}), bf16[4,40,1024]{2,1,0:T(8,128)(2,1)S(1)}, u32[]{:S(2)}, u32[]{:S(2)}) async-start(bf16[4,40,1024]{2,1,0:T(8,128)(2,1)} %bitcast.39), calls=%async_computation.5 | async-start | bytes 655360 | tf_op jit(solution)/shard_map/all_to_all | solution.py:64
Sparse Core Ops, SparseCore 0:
  22.0 33.2 all-gather.5
  66.1 40.3 reduce-scatter.6
  109.5 41.1 reduce-scatter.8
  153.5 40.9 all-gather.3
  203.5 37.8 reduce-scatter.10
  243.5 37.0 reduce-scatter.4
